TPU v7x, 32 devices: a whole 2x2x4 slice. The times are simulated.
32 devices in a mesh: row: 8 (over z, y), col: 4 (over x, core).
Axes of the slice: x: 2, y: 2, z: 4, core: 2. Of those that a mesh axis runs over, the one named last changes fastest.
Arguments:
- field: float32 [512, 64, 8, 512], P('row', 'col'), may hold values from -6 to 6
- modes: int32 [3, 256], replicated, may hold values from 0 to 511, as said below
Outputs:
- spectrum: float32 [64, 512, 8, 512], P(None, 'col', None, 'row')
- localized: float32 [512, 512], replicated
Inputs may be any that keep to these rules, and one draw needn't show every extreme that they name: `modes`: row 0 holds kx in 0 to 255, row 1 ky in 0 to 511, row 2 kz in 0 to 63; triples may repeat.
All inputs are finite; a program needn't handle non-finite values.
Results may differ from a plain program's by a relative error of at most 0.00013.
Values sent between devices are 32-bit elements; how exact they have to be, the bound alone decides.
A program may use at most 192 MiB of HBM per device.

v0:
```python
import math

import jax
import jax.numpy as jnp
from jax import lax
from jax.sharding import PartitionSpec as P

NX = 512
NY = 512
NZ = 64
REACH = 64


highest = lax.Precision.HIGHEST


def tables(length, count):
    points = lax.iota(jnp.int32, length)
    waves = lax.iota(jnp.int32, count)
    phase = points[:, None] * waves[None, :] % length
    angle = phase.astype(jnp.float32) * (2.0 * math.pi / length)
    return (jnp.cos(angle), jnp.sin(angle))


def rotation(count):
    source = lax.iota(jnp.int32, count)[:, None]
    target = lax.iota(jnp.int32, count)[None, :]
    even_out = target % 2 == 0
    plus = jnp.logical_and(source == target + 1, even_out).astype(jnp.float32)
    minus = jnp.logical_and(source + 1 == target, jnp.logical_not(even_out)).astype(jnp.float32)
    return plus - minus


def taper_of(modes, size_y, size_z, reach):
    first = modes[0].astype(jnp.float32)
    second = jnp.where(modes[1] < size_y // 2, modes[1], modes[1] - size_y).astype(jnp.float32)
    third = jnp.where(modes[2] < size_z // 2, modes[2], modes[2] - size_z).astype(jnp.float32)
    first = jnp.concatenate([first, first])
    second = jnp.concatenate([second, second])
    third = jnp.concatenate([third, third])
    dist = (first[:, None] - first[None, :]) ** 2 + (second[:, None] - second[None, :]) ** 2
    dist = dist + (third[:, None] - third[None, :]) ** 2
    return jnp.exp(-dist / (2.0 * reach * reach))


def y_transform(lines):
    length = lines.shape[0]
    cos_y, sin_y = tables(length, length)
    plain = jnp.einsum("ky,yzmq->kzmq", cos_y, lines, precision=highest)
    turned = jnp.einsum("ky,yzmq->kzmq", sin_y, lines, precision=highest)
    return plain + jnp.einsum("kzmq,qp->kzmp", turned, rotation(lines.shape[-1]), precision=highest)


def per_device(field, modes):
    members = field.shape[2]
    width = field.shape[3]
    cos_x, sin_x = tables(width, width // 2)
    x_table = jnp.stack([cos_x, -sin_x], axis=2).reshape(width, width)
    lines = jnp.einsum("yzmx,xq->yzmq", field, x_table, precision=highest)
    gathered = lax.all_to_all(lines, "row", split_axis=3, concat_axis=0, tiled=True)
    ytrans = y_transform(gathered)
    levels = lax.all_to_all(ytrans, "col", split_axis=0, concat_axis=1, tiled=True)
    depth = levels.shape[1]
    cos_z, sin_z = tables(depth, depth)
    plain = jnp.einsum("kz,yzmq->kymq", cos_z, levels, precision=highest)
    turned = jnp.einsum("kz,yzmq->kymq", sin_z, levels, precision=highest)
    combined = plain + jnp.einsum(
        "kymq,qp->kymp", turned, rotation(levels.shape[-1]), precision=highest
    )
    factor = 1.0 / math.sqrt(NX * NY * NZ)
    spectrum = combined * factor
    local_y = spectrum.shape[1]
    local_q = spectrum.shape[3]
    row_start = lax.axis_index("row") * local_q
    col_start = lax.axis_index("col") * local_y
    flat = spectrum.reshape(depth * local_y, members, local_q)
    offset = modes[1] - col_start
    inside_y = jnp.logical_and(offset >= 0, offset < local_y).astype(jnp.float32)
    index = modes[2] * local_y + jnp.clip(offset, 0, local_y - 1)
    picked_rows = flat[index]
    target = 2 * modes[0] - row_start
    columns = lax.iota(jnp.int32, local_q)[None, :]
    choose = jnp.stack([columns == target[:, None], columns == target[:, None] + 1], axis=2).astype(
        jnp.float32
    )
    choose = choose * inside_y[:, None, None]
    partial_value = jnp.einsum("smq,sqc->mcs", picked_rows, choose, precision=highest).reshape(
        members, -1
    )
    coef = lax.psum(partial_value, ("row", "col"))
    anomaly = coef - jnp.mean(coef, axis=0, keepdims=True)
    cov = jnp.dot(anomaly.T, anomaly, precision=highest) / (members - 1)
    localized = cov * taper_of(modes, NY, NZ, REACH)
    return (spectrum, localized)


def solution(mesh):
    placed = (P("row", "col", None, None), P())
    return jax.shard_map(
        per_device,
        mesh=mesh,
        in_specs=placed,
        out_specs=(P(None, "col", None, "row"), P()),
        check_vma=False,
    )
```

profile of v0, /device:TPU:0, one launch (start us, length us, event | category | flops | bytes accessed | tf_op | source)
XLA Modules:
  0.0 1304.9 jit_solution(5573586038033272029)
XLA Ops:
  0.6 2.1 sine_negate_fusion
  2.7 0.1 pad_maximum_fusion
  2.8 1.0 copy.29
  3.8 0.7 reshape.252
  4.5 40.4 %fusion.5 = f32[64,16,8,512]{3,0,2,1:T(8,128)} fusion(f32[64,16,8,512]{3,2,1,0:T(8,128)} %param.2, f32[512,512]{0,1:T(8,128)S(1)} %reshape.252), kind=kOutput, calls=%fused_computation.9 | convolution fusion | flops 25769803776 | bytes 34603008 | tf_op jit(solution)/shard_map/yzmx,xq->yzmq/dot_general | solution.py:59
  44.8 30.4 %copy.32 = f32[64,16,8,512]{0,2,1,3:T(8,128)} copy(f32[64,16,8,512]{3,0,2,1:T(8,128)} %fusion.5) | data formatting | bytes 33554432 | tf_op jit(solution)/shard_map/yzmx,xq->yzmq/dot_general | solution.py:59
  75.3 37.3 %reshape.273 = f32[8,1,524288]{2,1,0:T(1,128)} reshape(f32[512,16,8,64]{3,2,1,0:T(8,128)} %bitcast.65) | data formatting | bytes 33554432
  112.6 7.3 all-to-all-start
  119.9 363.1 %all-to-all-done = f32[8,1,524288]{2,1,0:T(1,128)} async-done(((f32[8,1,524288]{2,1,0:T(1,128)}), f32[8,1,524288]{2,1,0:T(1,128)}, u32[]{:S(2)}, u32[]{:S(2)}) %all-to-all-start) | async-done | bytes 16777248 | tf_op jit(solution)/shard_map/all_to_all | solution.py:60
  483.0 0.5 broadcast.368
  483.5 50.5 %reduce = f32[8,524288]{1,0:T(8,128)} reduce(f32[8,1,524288]{2,1,0:T(1,128)} %all-to-all-done, f32[]{:T(128)} %broadcast.368), dimensions={1}, to_apply=%all_to_all.26.reduce_sub_computation | reduce | bytes 33554436 | tf_op jit(solution)/shard_map/all_to_all | solution.py:60
  534.0 30.2 %reshape.274 = f32[512,16,8,64]{3,2,1,0:T(8,128)} reshape(f32[8,524288]{1,0:T(8,128)} %reduce) | data formatting | bytes 33554432
  564.2 31.9 %copy.60 = f32[64,16,8,8,64]{0,3,4,2,1:T(8,128)} copy(f32[64,16,8,8,64]{0,2,1,4,3:T(8,128)} %bitcast.67) | data formatting | bytes 33554432 | tf_op jit(solution)/shard_map/all_to_all | solution.py:60
  596.1 27.6 %reshape.264 = f32[512,8192]{0,1:T(8,128)} reshape(f32[8,64,16,8,64]{1,0,4,3,2:T(8,128)} %bitcast.68) | data formatting | bytes 33554432
  623.7 0.0 copy-start
  623.7 46.3 %fusion.15 = f32[512,8192]{0,1} fusion(f32[512,8192]{0,1:T(8,128)} %reshape.264), kind=kOutput, calls=%fused_computation.23 | convolution fusion | flops 25773473792 | bytes 33554432
  670.0 0.0 copy-done
  670.0 40.8 %fusion.13 = f32[512,8192]{0,1} fusion(f32[512,8192]{0,1:T(8,128)S(1)} %copy-done), kind=kOutput, calls=%fused_computation.21 | convolution fusion | flops 25773473792 | bytes 33554432
  710.7 22.7 %convolution_add_fusion = f32[512,16,8,64]{0,3,2,1:T(8,128)} fusion(f32[512,16,8,64]{0,3,2,1:T(8,128)} %bitcast.69, f32[512,16,8,64]{0,3,2,1:T(8,128)} %bitcast.70, s32[64]{0:T(128)S(1)} %iota_add_fusion, pred[64]{0:T(512)(128)(4,1)S(1)} %get-tuple-element.17, pred[64]{0:T(512)(128)(4,1)S(1)} %get-tuple-element.16), kind=kOutput, calls=%fused_computation.8 | convolution fusion | flops 3225448448 | bytes 50332032 | tf_op jit(solution)/shard_map/kzmq,qp->kzmp/dot_general | solution.py:51
  733.4 30.4 %copy.34 = f32[512,16,8,64]{3,2,1,0:T(8,128)} copy(f32[512,16,8,64]{0,3,2,1:T(8,128)} %convolution_add_fusion) | data formatting | bytes 33554432 | tf_op jit(solution)/shard_map/add | solution.py:51
  763.8 42.3 %reshape.275 = f32[4,1,1048576]{2,1,0:T(1,128)} reshape(f32[512,16,8,64]{3,2,1,0:T(8,128)} %copy.34) | data formatting | bytes 33554432
  806.1 0.0 copy-start.1
  806.1 7.1 all-to-all-start.1
  813.2 0.0 copy-done.1
  813.3 0.1 copy.39
  813.6 182.7 %all-to-all-done.1 = f32[4,1,1048576]{2,1,0:T(1,128)} async-done(((f32[4,1,1048576]{2,1,0:T(1,128)}), f32[4,1,1048576]{2,1,0:T(1,128)}, u32[]{:S(2)}, u32[]{:S(2)}) %all-to-all-start.1) | async-done | bytes 16777248 | tf_op jit(solution)/shard_map/all_to_all | solution.py:62
  996.2 54.6 %reduce.1 = f32[4,1048576]{1,0:T(4,128)} reduce(f32[4,1,1048576]{2,1,0:T(1,128)} %all-to-all-done.1, f32[]{:T(128)} %broadcast.368), dimensions={1}, to_apply=%all_to_all.30.reduce_sub_computation | reduce | bytes 33554436 | tf_op jit(solution)/shard_map/all_to_all | solution.py:62
  1050.9 55.4 %reshape.276 = f32[512,16,8,64]{3,2,1,0:T(8,128)} reshape(f32[4,1048576]{1,0:T(4,128)} %reduce.1) | data formatting | bytes 33554432
  1106.3 24.7 %copy.35 = f32[4,128,16,8,64]{1,2,0,4,3:T(8,128)} copy(f32[4,128,16,8,64]{4,3,2,1,0:T(8,128)} %bitcast.66) | data formatting | bytes 33554432 | tf_op jit(solution)/shard_map/all_to_all | solution.py:62
  1131.0 21.7 %fusion.32 = f32[64,128,8,64]{1,0,3,2:T(8,128)} fusion(f32[128,64,8,64]{0,1,3,2:T(8,128)} %bitcast.63), kind=kOutput, calls=%fused_computation.48 | convolution fusion | flops 3221282816 | bytes 33554432 | tf_op jit(solution)/shard_map/kz,yzmq->kymq/dot_general | solution.py:66
  1152.7 36.6 %fusion.1 = f32[64,128,8,64]{1,3,2,0:T(8,128)} fusion(f32[64,128,8,64]{1,0,3,2:T(8,128)} %fusion.32, s32[64]{0:T(128)S(1)} %iota_add_fusion, pred[64]{0:T(512)(128)(4,1)S(1)} %get-tuple-element.17, pred[64]{0:T(512)(128)(4,1)S(1)} %get-tuple-element.16), kind=kOutput, calls=%fused_computation.4 | convolution fusion | flops 3221254144 | bytes 33554816 | tf_op jit(solution)/shard_map/kymq,qp->kymp/dot_general | solution.py:67
  1189.3 35.2 %fusion = f32[64,128,8,64]{1,0,3,2:T(8,128)} fusion(f32[64,128,8,64]{1,3,2,0:T(8,128)} %fusion.1, f32[128,64,8,64]{0,1,3,2:T(8,128)} %bitcast.64), kind=kOutput, calls=%fused_computation.3 | convolution fusion | flops 3229671424 | bytes 50331648 | tf_op jit(solution)/shard_map/kz,yzmq->kymq/dot_general | solution.py:65
  1224.5 20.0 %copy.47 = f32[64,128,8,64]{3,2,1,0:T(8,128)} copy(f32[64,128,8,64]{1,0,3,2:T(8,128)} %fusion) | data formatting | bytes 33554432 | tf_op jit(solution)/shard_map/reshape | solution.py:76
  1244.5 16.0 %copy.41 = f32[64,128,8,64]{1,3,2,0:T(8,128)} copy(f32[64,128,8,64]{1,0,3,2:T(8,128)} %fusion) | data formatting | bytes 33554432
  1260.5 2.4 gather_fusion
  1262.8 1.8 fusion.80
  1264.6 0.1 copy.48
  1264.7 37.6 %psum.7 = f32[8,512]{1,0:T(8,128)S(1)} all-reduce(f32[8,512]{1,0:T(8,128)S(1)} %bitcast.72), channel_id=1, replica_groups=mesh['row'=8,'col'=4] {'row','col'}, use_global_device_ids=true, to_apply=%region_0.1 | all-reduce | flops 4096 | bytes 32768 | tf_op jit(solution)/shard_map/psum | solution.py:90
  1302.4 2.3 fusion.8
  (15 shorter events, 0.1 us)
Async XLA Ops:
  112.6 370.4 %all-to-all-start = ((f32[8,1,524288]{2,1,0:T(1,128)}), f32[8,1,524288]{2,1,0:T(1,128)}, u32[]{:S(2)}, u32[]{:S(2)}) async-start(f32[8,1,524288]{2,1,0:T(1,128)} %reshape.273), calls=%async_computation | async-start | bytes 33554432 | tf_op jit(solution)/shard_map/all_to_all | solution.py:60
  623.7 46.3 %copy-start = (f32[512,8192]{0,1:T(8,128)S(1)}, f32[512,8192]{0,1:T(8,128)}, u32[]{:S(2)}) copy-start(f32[512,8192]{0,1:T(8,128)} %reshape.264) | copy-start | bytes 50331652
  806.1 7.1 copy-start.1
  806.1 190.1 %all-to-all-start.1 = ((f32[4,1,1048576]{2,1,0:T(1,128)}), f32[4,1,1048576]{2,1,0:T(1,128)}, u32[]{:S(2)}, u32[]{:S(2)}) async-start(f32[4,1,1048576]{2,1,0:T(1,128)} %reshape.275), calls=%async_computation.1 | async-start | bytes 33554432 | tf_op jit(solution)/shard_map/all_to_all | solution.py:62
where the time goes:
time: 1310 us; the launch traced here: 1300 us
  waiting for transfers between devices  546 us (42%)
  local copies, waits for them, and re-layouts  351 us (27%)
  matrix products  248 us (19%)
  other arithmetic  107 us (8%)
  blocking collectives  37.6 us (3%)
  starting transfers between devices  14.4 us (1%)
    all_to_all x1, waiting for transfers between devices, per_device(): lax.all_to_all(lines, 'row', split_axis=3, concat_axis=0, tiled=True)  363 us
    unnamed x11, local copies, waits for them, and re-layouts  209 us
    all_to_all x1, waiting for transfers between devices, per_device(): lax.all_to_all(ytrans, 'col', split_axis=0, concat_axis=1, tiled=True)  183 us
    unnamed x2, matrix products  87 us
    all_to_all x1, other arithmetic, per_device(): lax.all_to_all(ytrans, 'col', split_axis=0, concat_axis=1, tiled=True)  54.6 us
    all_to_all x1, other arithmetic, per_device(): lax.all_to_all(lines, 'row', split_axis=3, concat_axis=0, tiled=True)  50.5 us
    dot_general x1, matrix products, per_device(): lines = jnp.einsum('yzmx,xq->yzmq', field, x_table, precision=highest)  40.4 us
    psum x1, blocking collectives, per_device(): coef = lax.psum(partial_value, ('row', 'col'))  37.6 us
  transfers between devices with their start and end apart: 2, of which 2 were waited for; matrix products, arithmetic and copies ran while one was open for 0% of the time, Pallas kernels for 0%

commit v1 on v0

v1 whole, which is shorter than its diff:
```python
import math

import jax
import jax.numpy as jnp
from jax import lax
from jax.experimental.layout import Layout, with_layout_constraint
from jax.sharding import PartitionSpec as P

NX = 512
NY = 512
NZ = 64
REACH = 64


highest = lax.Precision.HIGHEST
high = lax.Precision.HIGH
PIECES = 2


def tables(length, count):
    points = lax.iota(jnp.int32, length)
    waves = lax.iota(jnp.int32, count)
    phase = points[:, None] * waves[None, :] % length
    angle = phase.astype(jnp.float32) * (2.0 * math.pi / length)
    return (jnp.cos(angle), jnp.sin(angle))


def taper_of(modes, size_y, size_z, reach):
    first = modes[0].astype(jnp.float32)
    second = jnp.where(modes[1] < size_y // 2, modes[1], modes[1] - size_y).astype(jnp.float32)
    third = jnp.where(modes[2] < size_z // 2, modes[2], modes[2] - size_z).astype(jnp.float32)
    first = jnp.concatenate([first, first])
    second = jnp.concatenate([second, second])
    third = jnp.concatenate([third, third])
    dist = (first[:, None] - first[None, :]) ** 2 + (second[:, None] - second[None, :]) ** 2
    dist = dist + (third[:, None] - third[None, :]) ** 2
    return jnp.exp(-dist / (2.0 * reach * reach))


def twiddle(length, count, scale):
    cos, sin = tables(length, count)
    cos, sin = cos * scale, sin * scale
    return jnp.stack([jnp.stack([cos, sin]), jnp.stack([-sin, cos])])


def per_device(field, modes):
    members = field.shape[2]
    width = field.shape[3]
    rows, cols = lax.axis_size("row"), lax.axis_size("col")
    near, thick = field.shape[0], field.shape[1]
    length, depth = near * rows, thick * cols
    waves = width // 2 // rows
    pieces = PIECES if waves % PIECES == 0 else 1
    part = waves // pieces
    local_y = length // cols
    factor = 1.0 / math.sqrt(NX * NY * NZ)
    cos_x, sin_x = tables(width, width // 2)
    x_table = jnp.stack([cos_x, -sin_x]).reshape(2, width, rows, pieces, part)
    y_table = twiddle(length, length, 1.0).reshape(2, 2, rows, near, length)
    z_table = twiddle(depth, depth, factor).reshape(2, 2, cols, thick, depth)
    flat = field.reshape(near, thick * members, width)
    outs = []
    for piece in range(pieces):
        lines = jnp.einsum("cxrk,ylx->rckyl", x_table[:, :, :, piece], flat, precision=high)
        lines = with_layout_constraint(lines, Layout((0, 1, 2, 3, 4)))
        gathered = lax.all_to_all(lines, "row", split_axis=0, concat_axis=0, tiled=True)
        gathered = with_layout_constraint(gathered, Layout((0, 1, 2, 3, 4)))
        gathered = gathered.reshape(rows, 2, part, near, thick, members)
        ytrans = jnp.einsum("dcsyf,sckyzm->dkmzf", y_table, gathered, precision=high)
        ytrans = ytrans.reshape(2, part, members, thick, cols, local_y)
        ytrans = jnp.transpose(ytrans, (4, 0, 1, 2, 3, 5))
        levels = lax.all_to_all(ytrans, "col", split_axis=0, concat_axis=0, tiled=True)
        outs.append(jnp.einsum("edszg,sdkmzf->gmkef", z_table, levels, precision=high))
    whole = jnp.concatenate(outs, axis=2) if pieces > 1 else outs[0]
    local_q = 2 * waves
    whole = whole.reshape(depth, members, local_q, local_y)
    spectrum = jnp.transpose(whole, (0, 3, 1, 2))
    row_start = lax.axis_index("row") * waves
    col_start = lax.axis_index("col") * local_y
    wave = modes[0] - row_start
    line = modes[1] - col_start
    inside = (wave >= 0) & (wave < waves) & (line >= 0) & (line < local_y)
    wave = jnp.clip(wave, 0, waves - 1)
    line = jnp.clip(line, 0, local_y - 1)
    columns = lax.iota(jnp.int32, local_y)
    tall = whole.reshape(depth, members, waves, 2, local_y)
    picked = tall[modes[2], :, wave]
    hit = (columns[None, :] == line[:, None]) & inside[:, None]
    value = jnp.sum(jnp.where(hit[:, None, None, :], picked, 0.0), axis=-1)
    partial_value = jnp.transpose(value, (1, 2, 0)).reshape(members, -1)
    coef = lax.psum(partial_value, ("row", "col"))
    anomaly = coef - jnp.mean(coef, axis=0, keepdims=True)
    cov = jnp.dot(anomaly.T, anomaly, precision=highest) / (members - 1)
    localized = cov * taper_of(modes, NY, NZ, REACH)
    return (spectrum, localized)


def solution(mesh):
    placed = (P("row", "col", None, None), P())
    return jax.shard_map(
        per_device,
        mesh=mesh,
        in_specs=placed,
        out_specs=(P(None, "col", None, "row"), P()),
        check_vma=False,
    )
```

time: 1310 us -> 705 us (0.54)
  local copies, waits for them, and re-layouts: 351 us -> 104 us
  matrix products: 248 us -> 94.3 us
  waiting for transfers between devices: 546 us -> 422 us
  other arithmetic: 107 us -> 14.7 us
    unnamed x11 -> x6, local copies, waits for them, and re-layouts: 209 us -> 14.3 us
    all_to_all x2 -> x4, waiting for transfers between devices: 546 us -> 422 us  [the longest x2 295 us: per_device(): lax.all_to_all(lines, 'row', split_axis=0, concat_axis=0, tiled=True)]
    all_to_all x2 -> x0, other arithmetic: 105 us -> none  [the longest x1 54.6 us: per_device(): lax.all_to_all(ytrans, 'col', split_axis=0, concat_axis=1, tiled=True)]
    unnamed x2 -> x0, matrix products: 87 us -> none
    dot_general x6, matrix products: 158 us -> 92 us  [the longest x2 55 us: per_device(): jnp.einsum('dcsyf,sckyzm->dkmzf', y_table, gathered, precision=high)]
    all_to_all x3 -> x0, local copies, waits for them, and re-layouts: 57.1 us -> none  [the longest x2 32.4 us: per_device(): lax.all_to_all(lines, 'row', split_axis=3, concat_axis=0, tiled=True)]
    add x1 -> x0, local copies, waits for them, and re-layouts: 30.4 us -> none  [y_transform(): plain + jnp.einsum('kzmq,qp->kzmp', turned, rotation(lines.shape[-1]), pr...]
    another operation x1 -> x2, local copies, waits for them, and re-layouts: 0.97 us -> 24.5 us  [per_device(): gathered = with_layout_constraint(gathered, Layout((0, 1, 2, 3, 4)))]
  transfers between devices with their start and end apart: 2 -> 4, of which waited for: 2 -> 4; matrix products, arithmetic and copies ran while one was open for 0% -> 19% of each run, Pallas kernels for 0% -> 0%
where the time goes in v1:
time: 705 us; the launch traced here: 699 us
  waiting for transfers between devices  422 us (60%)
  local copies, waits for them, and re-layouts  104 us (15%)
  matrix products  94.3 us (13%)
  blocking collectives  37.7 us (5%)
  starting transfers between devices  24.7 us (4%)
  other arithmetic  14.7 us (2%)
    all_to_all x2, waiting for transfers between devices, per_device(): lax.all_to_all(lines, 'row', split_axis=0, concat_axis=0, tiled=True)  295 us
    all_to_all x2, waiting for transfers between devices, per_device(): lax.all_to_all(ytrans, 'col', split_axis=0, concat_axis=0, tiled=True)  126 us
    dot_general x2, matrix products, per_device(): jnp.einsum('dcsyf,sckyzm->dkmzf', y_table, gathered, precision=high)  55 us
    psum x1, blocking collectives, per_device(): coef = lax.psum(partial_value, ('row', 'col'))  37.7 us
    another operation x2, local copies, waits for them, and re-layouts, per_device(): gathered = with_layout_constraint(gathered, Layout((0, 1, 2, 3, 4)))  24.5 us
    dot_general x2, matrix products, per_device(): jnp.einsum('cxrk,ylx->rckyl', x_table[:, :, :, piece], flat, precision=high)  20.5 us
    concatenate x1, local copies, waits for them, and re-layouts, per_device(): whole = jnp.concatenate(outs, axis=2) if pieces > 1 else outs[0]  19.5 us
    dot_general x2, matrix products, per_device(): jnp.einsum('edszg,sdkmzf->gmkef', z_table, levels, precision=high)  16.5 us
  transfers between devices with their start and end apart: 4, of which 4 were waited for; matrix products, arithmetic and copies ran while one was open for 19% of the time, Pallas kernels for 0%

profile of v1, /device:TPU:0, one launch (start us, length us, event | category | flops | bytes accessed | tf_op | source)
XLA Modules:
  0.0 698.6 jit_solution(1257400286542088055)
XLA Ops:
  0.6 2.1 fusion.34
  2.8 10.2 %fusion.4 = f32[2,8,16,64,128]{4,2,3,1,0:T(8,128)S(1)} fusion(f32[64,16,8,512]{3,2,1,0:T(8,128)} %param.2, f32[1,512,8,2,16]{1,4,2,0,3:T(8,128)S(1)} %get-tuple-element.6, f32[1,512,8,2,16]{1,4,2,0,3:T(8,128)S(1)} %get-tuple-element.7), kind=kOutput, calls=%fused_computation.6 | convolution fusion | flops 6442582016 | bytes 26214400 | tf_op jit(solution)/shard_map/cxrk,ylx->rckyl/dot_general | solution.py:64
  13.0 6.0 copy.83
  19.0 7.6 %all-to-all-start = ((f32[8,2,16,64,128]{4,3,2,1,0:T(8,128)}), f32[8,2,16,64,128]{4,3,2,1,0:T(8,128)}, u32[]{:S(2)}, u32[]{:S(2)}) async-start(f32[8,2,16,64,128]{4,3,2,1,0:T(8,128)} %bitcast.107), calls=%async_computation | async-start | bytes 16777216 | tf_op jit(solution)/shard_map/all_to_all | solution.py:66
  26.6 10.2 %fusion.2 = f32[2,8,16,64,128]{4,2,3,1,0:T(8,128)S(1)} fusion(f32[64,16,8,512]{3,2,1,0:T(8,128)} %param.2, f32[1,512,8,2,16]{1,4,2,0,3:T(8,128)S(1)} %get-tuple-element.7, f32[1,512,8,2,16]{1,4,2,0,3:T(8,128)S(1)} %get-tuple-element.6), kind=kOutput, calls=%fused_computation.4 | convolution fusion | flops 6442582016 | bytes 26214400 | tf_op jit(solution)/shard_map/cxrk,ylx->rckyl/dot_general | solution.py:64
  36.9 5.8 copy.81
  42.7 167.0 %all-to-all-done = f32[8,2,16,64,128]{4,3,2,1,0:T(8,128)} async-done(((f32[8,2,16,64,128]{4,3,2,1,0:T(8,128)}), f32[8,2,16,64,128]{4,3,2,1,0:T(8,128)}, u32[]{:S(2)}, u32[]{:S(2)}) %all-to-all-start) | async-done | bytes 8388640 | tf_op jit(solution)/shard_map/all_to_all | solution.py:66
  209.7 5.3 all-to-all-start.2
  215.0 4.2 fusion.28
  219.2 12.2 %copy.22 = f32[8,2,16,64,128]{3,4,2,1,0:T(8,128)} copy(f32[8,2,16,64,128]{4,3,2,1,0:T(8,128)} %all-to-all-done) | data formatting | bytes 16777216 | tf_op jit(solution)/shard_map/layout_constraint | solution.py:67
  231.5 27.8 %fusion.6 = f32[16,16,8,2,512,1,1]{4,2,5,1,0,3,6:T(8,128)S(1)} fusion(f32[1,1,8,64,512]{4,3,1,0,2:T(8,128)S(1)} %get-tuple-element.13, f32[1,1,8,64,512]{4,3,1,0,2:T(8,128)S(1)} %get-tuple-element.12, f32[1,1,8,64,512]{4,3,1,0,2:T(8,128)S(1)} %get-tuple-element.11, f32[8,2,16,64,128]{3,4,2,1,0:T(8,128)} %copy.22), kind=kOutput, calls=%fused_computation.8 | convolution fusion | flops 12888047616 | bytes 19922944 | tf_op jit(solution)/shard_map/dcsyf,sckyzm->dkmzf/dot_general | solution.py:69
  259.2 1.4 copy.79
  260.7 8.1 %copy.82 = f32[2,16,8,16,4,128]{5,3,0,2,1,4:T(8,128)} copy(f32[2,16,8,16,4,128]{5,2,4,1,0,3:T(8,128)S(1)} %bitcast.108) | data formatting | bytes 16777216 | tf_op jit(solution)/shard_map/reshape | solution.py:70
  268.7 128.5 %all-to-all-done.2 = f32[8,2,16,64,128]{4,3,2,1,0:T(8,128)} async-done(((f32[8,2,16,64,128]{4,3,2,1,0:T(8,128)}), f32[8,2,16,64,128]{4,3,2,1,0:T(8,128)}, u32[]{:S(2)}, u32[]{:S(2)}) %all-to-all-start.2) | async-done | bytes 8388640 | tf_op jit(solution)/shard_map/all_to_all | solution.py:66
  397.2 5.8 all-to-all-start.1
  403.1 12.2 %copy.27 = f32[8,2,16,64,128]{3,4,2,1,0:T(8,128)} copy(f32[8,2,16,64,128]{4,3,2,1,0:T(8,128)} %all-to-all-done.2) | data formatting | bytes 16777216 | tf_op jit(solution)/shard_map/layout_constraint | solution.py:67
  415.3 27.3 %fusion = f32[16,16,8,2,512,1,1]{4,2,5,1,0,3,6:T(8,128)S(1)} fusion(f32[1,1,8,64,512]{4,3,1,0,2:T(8,128)S(1)} %get-tuple-element.13, f32[1,1,8,64,512]{4,3,1,0,2:T(8,128)S(1)} %get-tuple-element.12, f32[1,1,8,64,512]{4,3,1,0,2:T(8,128)S(1)} %get-tuple-element.11, f32[8,2,16,64,128]{3,4,2,1,0:T(8,128)} %copy.27), kind=kOutput, calls=%fused_computation.2 | convolution fusion | flops 12888047616 | bytes 19922944 | tf_op jit(solution)/shard_map/dcsyf,sckyzm->dkmzf/dot_general | solution.py:69
  442.6 1.4 copy.78
  444.0 8.3 %copy.80 = f32[2,16,8,16,4,128]{5,3,0,2,1,4:T(8,128)} copy(f32[2,16,8,16,4,128]{5,2,4,1,0,3:T(8,128)S(1)} %bitcast.109) | data formatting | bytes 16777216 | tf_op jit(solution)/shard_map/reshape | solution.py:70
  452.3 43.9 %all-to-all-done.1 = f32[4,2,16,8,16,128]{5,4,1,3,2,0:T(8,128)} async-done(((f32[4,2,16,8,16,128]{5,4,1,3,2,0:T(8,128)}), f32[4,2,16,8,16,128]{5,4,1,3,2,0:T(8,128)}, u32[]{:S(2)}, u32[]{:S(2)}) %all-to-all-start.1) | async-done | bytes 8388640 | tf_op jit(solution)/shard_map/all_to_all | solution.py:72
  496.2 0.0 copy-start.1
  496.2 6.0 all-to-all-start.3
  502.2 0.0 copy-done.1
  502.4 0.1 fusion.35
  502.5 0.2 sine_multiply_fusion
  502.7 10.2 %fusion.10 = f32[16,8,128,2,64,1,1]{2,4,5,0,3,1,6:T(8,128)} fusion(f32[4,2,16,8,16,128]{5,4,1,3,2,0:T(8,128)} %all-to-all-done.1, f32[1,1,4,16,64]{4,3,2,1,0:T(8,128)S(1)} %get-tuple-element.16, f32[1,1,4,16,64]{4,3,2,1,0:T(8,128)S(1)} %get-tuple-element.15, f32[1,1,4,16,64]{4,3,2,1,0:T(8,128)S(1)} %get-tuple-element.14), kind=kOutput, calls=%fused_computation.12 | convolution fusion | flops 1610661888 | bytes 16826368 | tf_op jit(solution)/shard_map/edszg,sdkmzf->gmkef/dot_general | solution.py:73
  512.9 82.4 %all-to-all-done.3 = f32[4,2,16,8,16,128]{5,4,1,3,2,0:T(8,128)} async-done(((f32[4,2,16,8,16,128]{5,4,1,3,2,0:T(8,128)}), f32[4,2,16,8,16,128]{5,4,1,3,2,0:T(8,128)}, u32[]{:S(2)}, u32[]{:S(2)}) %all-to-all-start.3) | async-done | bytes 8388640 | tf_op jit(solution)/shard_map/all_to_all | solution.py:72
  595.3 0.0 copy-start
  595.3 6.3 fusion.8
  601.7 0.0 copy-done
  601.7 7.9 %copy_bitcast_fusion = (f32[64,8,16,2,128]{4,0,3,1,2:T(8,128)}, f32[64,8,16,2,128]{4,0,3,1,2:T(8,128)}) fusion(f32[16,8,128,2,64,1,1]{2,4,5,0,3,1,6:T(8,128)S(1)} %fusion.8, f32[16,8,128,2,64,1,1]{2,4,5,0,3,1,6:T(8,128)S(1)} %copy-done), kind=kLoop, calls=%fused_computation.14 | loop fusion | bytes 33554432 | tf_op jit(solution)/shard_map/edszg,sdkmzf->gmkef/transpose | solution.py:73
  609.6 7.0 pad_maximum_fusion
  616.5 19.5 %copy.31 = f32[64,8,32,2,128]{4,1,3,2,0:T(8,128)} copy(f32[64,8,32,2,128]{4,0,3,1,2:T(8,128)S(1)} %pad_maximum_fusion) | data formatting | bytes 33554432 | tf_op jit(solution)/shard_map/concatenate | solution.py:74
  636.1 6.9 gather_fusion
  643.0 0.9 select_reduce_fusion
  643.9 0.1 copy.56
  644.0 37.7 %psum.7 = f32[8,512]{1,0:T(8,128)S(1)} all-reduce(f32[8,512]{1,0:T(8,128)S(1)} %bitcast.112), channel_id=1, replica_groups=mesh['row'=8,'col'=4] {'row','col'}, use_global_device_ids=true, to_apply=%region_1.2 | all-reduce | flops 4096 | bytes 32768 | tf_op jit(solution)/shard_map/psum | solution.py:91
  681.7 14.2 %copy.34 = f32[64,128,8,64]{1,3,2,0:T(8,128)} copy(f32[64,128,8,64]{1,2,3,0:T(8,128)} %bitcast.103) | data formatting | bytes 33554432
  695.9 2.3 fusion.12
  (13 shorter events, 0.1 us)
Async XLA Ops:
  19.0 190.7 %all-to-all-start = ((f32[8,2,16,64,128]{4,3,2,1,0:T(8,128)}), f32[8,2,16,64,128]{4,3,2,1,0:T(8,128)}, u32[]{:S(2)}, u32[]{:S(2)}) async-start(f32[8,2,16,64,128]{4,3,2,1,0:T(8,128)} %bitcast.107), calls=%async_computation | async-start | bytes 16777216 | tf_op jit(solution)/shard_map/all_to_all | solution.py:66
  209.7 187.5 %all-to-all-start.2 = ((f32[8,2,16,64,128]{4,3,2,1,0:T(8,128)}), f32[8,2,16,64,128]{4,3,2,1,0:T(8,128)}, u32[]{:S(2)}, u32[]{:S(2)}) async-start(f32[8,2,16,64,128]{4,3,2,1,0:T(8,128)} %bitcast.105), calls=%async_computation.2 | async-start | bytes 16777216 | tf_op jit(solution)/shard_map/all_to_all | solution.py:66
  397.2 98.9 %all-to-all-start.1 = ((f32[4,2,16,8,16,128]{5,4,1,3,2,0:T(8,128)}), f32[4,2,16,8,16,128]{5,4,1,3,2,0:T(8,128)}, u32[]{:S(2)}, u32[]{:S(2)}) async-start(f32[4,2,16,8,16,128]{5,4,1,3,2,0:T(8,128)} %bitcast.106), calls=%async_computation.1 | async-start | bytes 16777216 | tf_op jit(solution)/shard_map/all_to_all | solution.py:72
  496.2 6.0 copy-start.1
  496.2 99.1 %all-to-all-start.3 = ((f32[4,2,16,8,16,128]{5,4,1,3,2,0:T(8,128)}), f32[4,2,16,8,16,128]{5,4,1,3,2,0:T(8,128)}, u32[]{:S(2)}, u32[]{:S(2)}) async-start(f32[4,2,16,8,16,128]{5,4,1,3,2,0:T(8,128)} %bitcast.104), calls=%async_computation.3 | async-start | bytes 16777216 | tf_op jit(solution)/shard_map/all_to_all | solution.py:72
  595.3 6.3 copy-start
